TPU v7x, 32 devices: a whole 2x2x4 slice. The times are simulated.
32 devices in a mesh: bead: 8 (over z, core), atom: 4 (over y, x).
Axes of the slice: x: 2, y: 2, z: 4, core: 2. Of those that a mesh axis runs over, the one named last changes fastest.
Arguments:
- positions: float32 [32, 3, 4096], P('bead', None, 'atom'), may hold values from -6 to 6
- momenta: float32 [32, 3, 4096], P('bead', None, 'atom'), may hold values from -6 to 6
- charge: float32 [4096], P('atom'), may hold values from -1 to 1
- masses: float32 [4096], P('atom'), may hold values from 0.5 to 4
- pair_local: int32 [128], P('atom'), may hold values from 0 to 31, as said below
- pair_other: int32 [128], P('atom'), may hold values from 0 to 31, as said below
- pair_count: int32 [4], P('atom'), may hold values from 0 to 32, as said below
Outputs:
- new_positions: float32 [32, 3, 4096], P('bead', None, 'atom')
- new_momenta: float32 [32, 3, 4096], P('bead', None, 'atom')
- spring: float32 [4096], P('atom')
Inputs may be any that keep to these rules, and one draw needn't show every extreme that they name: `pair_local`: the slots of atom block d (slots d * 32 to (d + 1) * 32 - 1) name tiles of that block: d * 8 to (d + 1) * 8 - 1. `pair_other`: each slot's neighbour tile lies within 8 tiles of its tile, counting cyclically over 32 tiles. `pair_count`: the counts of blocks d and d + 2 sum to at most 32.
All inputs are finite; a program needn't handle non-finite values.
Results may differ from a plain program's by a relative error of at most 0.000071.
Values sent between devices are 32-bit elements; how exact they have to be, the bound alone decides.
A program may use at most 64 MiB of HBM per device.

v0:
```python
import jax
import jax.numpy as jnp
from jax import lax
from jax.sharding import PartitionSpec as P

time_step = 1.0
omega_cycle = 1.2
width_sq = 2.0


def extended(block, sides, width):
    for axis, dim in sides:
        count = lax.axis_size(axis)
        forward = [(i, i + 1) for i in range(count - 1)]
        forward.append((count - 1, 0))
        backward = [(target, source) for source, target in forward]
        low = lax.ppermute(
            lax.slice_in_dim(block, block.shape[dim] - width, None, axis=dim), axis, forward
        )
        high = lax.ppermute(lax.slice_in_dim(block, 0, width, axis=dim), axis, backward)
        block = jnp.concatenate([low, block, high], axis=dim)
    return block


def cycle_table(beads):
    bead_index = jnp.arange(beads, dtype=jnp.float32)[:, None]
    mode_index = jnp.arange(beads, dtype=jnp.float32)[None, :]
    middle = beads // 2
    angle = 2.0 * jnp.pi * bead_index * mode_index / beads
    cosine_part = jnp.sqrt(2.0 / beads) * jnp.cos(angle)
    sine_part = jnp.sqrt(2.0 / beads) * jnp.sin(angle)
    edge_part = jnp.sqrt(1.0 / beads) * jnp.cos(jnp.pi * bead_index)
    first = jnp.sqrt(1.0 / beads) * jnp.ones_like(angle)
    table = jnp.where(
        mode_index == 0,
        first,
        jnp.where(
            mode_index < middle, cosine_part, jnp.where(mode_index == middle, edge_part, sine_part)
        ),
    )
    frequency = 2.0 * omega_cycle * jnp.sin(jnp.pi * jnp.arange(beads, dtype=jnp.float32) / beads)
    return (table, frequency)


def pair_force(left_pos, right_pos, left_charge, right_charge):
    separation = left_pos[..., :, None] - right_pos[..., None, :]
    dist_sq = jnp.sum(separation * separation, axis=-3)
    weights = (
        left_charge[..., :, None]
        * right_charge[..., None, :]
        * jnp.exp(-dist_sq / (2.0 * width_sq))
        / width_sq
    )
    return jnp.sum(separation * weights[..., None, :, :], axis=-1)


def propagate(mode_pos, mode_mom, frequency, masses, beads):
    freq_col = frequency[:, None, None]
    mass_row = masses[None, None, :]
    cosine = jnp.cos(freq_col * time_step)
    sine = jnp.sin(freq_col * time_step)
    reach = jnp.where(freq_col > 0, sine / jnp.where(freq_col > 0, freq_col, 1.0), time_step)
    moved_pos = cosine * mode_pos + reach * mode_mom / mass_row
    moved_mom = -mass_row * freq_col * sine * mode_pos + cosine * mode_mom
    spring = (
        jnp.sum(0.5 * mass_row * freq_col * freq_col * moved_pos * moved_pos, axis=(0, 1)) / beads
    )
    return (moved_pos, moved_mom, spring)


def slot_forces(packed):
    slots = packed.shape[0]
    blocks = packed.reshape((slots // 4, 4) + packed.shape[1:])

    def one_block(block_pack):
        return pair_force(
            block_pack[:, 0, :, :3],
            block_pack[:, 1, :, :3],
            block_pack[:, 0, :, 3],
            block_pack[:, 1, :, 3],
        )

    result = lax.map(one_block, blocks)
    return result.reshape((slots,) + result.shape[2:])


def on_device(positions, momenta, charge, masses, pair_local, pair_other, pair_count):
    bead_dev, _, atom_dev = positions.shape
    tile_atoms = 128
    tile_dev = atom_dev // tile_atoms
    atom_count = lax.axis_size("atom")
    bead_count = lax.axis_size("bead")
    beads = bead_dev * bead_count
    tiles = tile_dev * atom_count
    slots = pair_local.shape[0]
    hp = lax.Precision.HIGHEST
    table, frequency = cycle_table(beads)
    sub_atoms = atom_dev // bead_count
    gathered_pos = lax.all_to_all(positions, "bead", split_axis=2, concat_axis=0, tiled=True)
    charge_rows = jnp.broadcast_to(charge[None, None, :], (bead_dev, 1, atom_dev))
    packed = jnp.concatenate([positions, charge_rows], axis=1)
    haloed = extended(packed, (("atom", 2),), atom_dev)
    ext_tiles = jnp.transpose(haloed.reshape(bead_dev, 4, 3 * tile_dev, tile_atoms), (2, 0, 1, 3))
    base_tile = lax.axis_index("atom") * tile_dev - tile_dev
    left_local = (pair_local - base_tile) % tiles
    right_local = (pair_other - base_tile) % tiles
    live_count = pair_count[0]
    slot_ids = jnp.arange(slots)
    live_mask = (slot_ids < live_count).astype(jnp.float32)
    left_block = jnp.take(ext_tiles, left_local, axis=0)
    right_block = jnp.take(ext_tiles, right_local, axis=0)
    left_block = jnp.concatenate(
        [left_block[:, :, :3], left_block[:, :, 3:] * live_mask[:, None, None, None]], axis=2
    )
    forces = slot_forces(jnp.stack([left_block, right_block], axis=1))
    onehot = (left_local[None, :] - tile_dev == jnp.arange(tile_dev)[:, None]).astype(jnp.float32)
    summed = jnp.einsum("ts,sbca->bcta", onehot, forces, precision=hp)
    force = summed.reshape(bead_dev, 3, atom_dev)
    kicked = momenta + 0.5 * time_step * force
    gathered_mom = lax.all_to_all(kicked, "bead", split_axis=2, concat_axis=0, tiled=True)
    mode_pos = jnp.einsum("jk,jca->kca", table, gathered_pos, precision=hp)
    mode_mom = jnp.einsum("jk,jca->kca", table, gathered_mom, precision=hp)
    sub_masses = lax.dynamic_slice_in_dim(masses, lax.axis_index("bead") * sub_atoms, sub_atoms, 0)
    moved_pos, moved_mom, spring_sub = propagate(mode_pos, mode_mom, frequency, sub_masses, beads)
    stacked = jnp.stack([moved_pos, moved_mom], axis=1)
    returned_rows = jnp.einsum("jk,kxca->jxca", table, stacked, precision=hp)
    result = lax.all_to_all(returned_rows, "bead", split_axis=0, concat_axis=3, tiled=True)
    spring = lax.all_gather(spring_sub, "bead", axis=0, tiled=True)
    return (result[:, 0], result[:, 1], spring)


def solution(mesh):
    return jax.shard_map(
        on_device,
        mesh=mesh,
        in_specs=(
            P("bead", None, "atom"),
            P("bead", None, "atom"),
            P("atom"),
            P("atom"),
            P("atom"),
            P("atom"),
            P("atom"),
        ),
        out_specs=(P("bead", None, "atom"), P("bead", None, "atom"), P("atom")),
        check_vma=False,
    )
```

profile of v0, /device:TPU:0, one launch (start us, length us, event | category | flops | bytes accessed | tf_op | source)
XLA Modules:
  0.0 81.9 jit_solution(6459633473460166946)
XLA Ops:
  1.3 0.8 pad_maximum_fusion.3
  2.2 3.0 %collective-permute-start = (f32[4,4,1024]{2,0,1:T(4,128)S(1)}, f32[4,4,1024]{2,0,1:T(4,128)S(1)}, u32[]{:S(2)}, u32[]{:S(2)}) collective-permute-start(f32[4,4,1024]{2,0,1:T(4,128)S(1)} %pad_maximum_fusion.3), channel_id=1, source_target_pairs={{0,1},{1,2},{2,3},{3,0},{4,5},{5,6},{6,7},{7,4},{8,9},{9,10},{10,1... | collective-permute-start | bytes 196616 | tf_op jit(solution)/shard_map/ppermute | solution.py:17
  5.2 1.0 %collective-permute-start.1 = (f32[4,4,1024]{2,0,1:T(4,128)S(1)}, f32[4,4,1024]{2,0,1:T(4,128)S(1)}, u32[]{:S(2)}, u32[]{:S(2)}) collective-permute-start(f32[4,4,1024]{2,0,1:T(4,128)S(1)} %pad_maximum_fusion.3), channel_id=1, source_target_pairs={{1,0},{2,1},{3,2},{0,3},{5,4},{6,5},{7,6},{4,7},{9,8},{10,9},{11,1... | collective-permute-start | bytes 196616 | tf_op jit(solution)/shard_map/ppermute | solution.py:20
  6.2 1.6 %copy.64 = f32[4,3,1024]{0,1,2:T(4,128)S(1)} copy(f32[4,3,1024]{2,0,1:T(4,128)} %param.11) | data formatting | bytes 98304 | tf_op args[0]
  7.8 1.9 %reshape.224 = f32[8,1,1536]{2,1,0:T(1,128)} reshape(f32[1024,3,4]{2,1,0:T(4,128)S(1)} %bitcast.89) | data formatting | bytes 98304
  9.7 5.3 %all-to-all-start = ((f32[8,1,1536]{2,1,0:T(1,128)}), f32[8,1,1536]{2,1,0:T(1,128)S(1)}, u32[]{:S(2)}, u32[]{:S(2)}) async-start(f32[8,1,1536]{2,1,0:T(1,128)} %reshape.224), calls=%async_computation | async-start | bytes 98304 | tf_op jit(solution)/shard_map/all_to_all | solution.py:99
  16.0 0.8 broadcast_multiply_fusion
  19.4 27.1 %while.10 = (s32[]{:T(128)}, f32[8,4,4,3,128]{4,3,2,1,0:T(4,128)S(1)}, f32[8,4,2,4,4,128]{5,3,1,4,2,0:T(4,128)S(1)}, s32[]{:T(128)}) while((s32[]{:T(128)}, f32[8,4,4,3,128]{4,3,2,1,0:T(4,128)S(1)}, f32[8,4,2,4,4,128]{5,3,1,4,2,0:T(4,128)S(1)}, s32[]{:T(128)}) %tuple.40), condition=%wide.region_3.5_spmd, body=%wide.region_0.4_spmd.sunk | while | flops 5761026 | bytes 4759613 | solution.py:83
  19.5 1.0 %fusion.62 = f32[4,4,128,128]{3,2,1,0:T(8,128)S(1)} fusion(f32[4,4,3,128]{3,2,1,0:T(4,128)S(1)} %copy.92, f32[4,4,3,128]{3,2,1,0:T(4,128)S(1)} %copy.93), kind=kLoop, calls=%fused_computation.4.clone.1 | loop fusion | flops 2097152 | bytes 1097728 | tf_op jit(solution)/shard_map/while/body/eval_jaxpr/reduce_sum | solution.py:47
  20.9 1.9 %fusion.63 = f32[4,4,3,128]{3,2,1,0:T(4,128)S(1)} fusion(f32[4,4,128,128]{3,2,1,0:T(8,128)S(1)} %multiply_multiply_fusion.5, f32[4,4,3,128]{3,2,1,0:T(4,128)S(1)} %copy.92, f32[4,4,3,128]{3,2,1,0:T(4,128)S(1)} %copy.93), kind=kLoop, calls=%fused_computation.5.clone.1 | loop fusion | flops 2353152 | bytes 1122304 | tf_op jit(solution)/shard_map/while/body/eval_jaxpr/reduce_sum | solution.py:54
  22.9 1.0 %fusion.62 = f32[4,4,128,128]{3,2,1,0:T(8,128)S(1)} fusion(f32[4,4,3,128]{3,2,1,0:T(4,128)S(1)} %copy.92, f32[4,4,3,128]{3,2,1,0:T(4,128)S(1)} %copy.93), kind=kLoop, calls=%fused_computation.4.clone.1 | loop fusion | flops 2097152 | bytes 1097728 | tf_op jit(solution)/shard_map/while/body/eval_jaxpr/reduce_sum | solution.py:47
  24.3 1.9 %fusion.63 = f32[4,4,3,128]{3,2,1,0:T(4,128)S(1)} fusion(f32[4,4,128,128]{3,2,1,0:T(8,128)S(1)} %multiply_multiply_fusion.5, f32[4,4,3,128]{3,2,1,0:T(4,128)S(1)} %copy.92, f32[4,4,3,128]{3,2,1,0:T(4,128)S(1)} %copy.93), kind=kLoop, calls=%fused_computation.5.clone.1 | loop fusion | flops 2353152 | bytes 1122304 | tf_op jit(solution)/shard_map/while/body/eval_jaxpr/reduce_sum | solution.py:54
  26.3 1.0 %fusion.62 = f32[4,4,128,128]{3,2,1,0:T(8,128)S(1)} fusion(f32[4,4,3,128]{3,2,1,0:T(4,128)S(1)} %copy.92, f32[4,4,3,128]{3,2,1,0:T(4,128)S(1)} %copy.93), kind=kLoop, calls=%fused_computation.4.clone.1 | loop fusion | flops 2097152 | bytes 1097728 | tf_op jit(solution)/shard_map/while/body/eval_jaxpr/reduce_sum | solution.py:47
  27.7 1.9 %fusion.63 = f32[4,4,3,128]{3,2,1,0:T(4,128)S(1)} fusion(f32[4,4,128,128]{3,2,1,0:T(8,128)S(1)} %multiply_multiply_fusion.5, f32[4,4,3,128]{3,2,1,0:T(4,128)S(1)} %copy.92, f32[4,4,3,128]{3,2,1,0:T(4,128)S(1)} %copy.93), kind=kLoop, calls=%fused_computation.5.clone.1 | loop fusion | flops 2353152 | bytes 1122304 | tf_op jit(solution)/shard_map/while/body/eval_jaxpr/reduce_sum | solution.py:54
  29.7 1.0 %fusion.62 = f32[4,4,128,128]{3,2,1,0:T(8,128)S(1)} fusion(f32[4,4,3,128]{3,2,1,0:T(4,128)S(1)} %copy.92, f32[4,4,3,128]{3,2,1,0:T(4,128)S(1)} %copy.93), kind=kLoop, calls=%fused_computation.4.clone.1 | loop fusion | flops 2097152 | bytes 1097728 | tf_op jit(solution)/shard_map/while/body/eval_jaxpr/reduce_sum | solution.py:47
  31.1 1.9 %fusion.63 = f32[4,4,3,128]{3,2,1,0:T(4,128)S(1)} fusion(f32[4,4,128,128]{3,2,1,0:T(8,128)S(1)} %multiply_multiply_fusion.5, f32[4,4,3,128]{3,2,1,0:T(4,128)S(1)} %copy.92, f32[4,4,3,128]{3,2,1,0:T(4,128)S(1)} %copy.93), kind=kLoop, calls=%fused_computation.5.clone.1 | loop fusion | flops 2353152 | bytes 1122304 | tf_op jit(solution)/shard_map/while/body/eval_jaxpr/reduce_sum | solution.py:54
  33.0 1.0 %fusion.62 = f32[4,4,128,128]{3,2,1,0:T(8,128)S(1)} fusion(f32[4,4,3,128]{3,2,1,0:T(4,128)S(1)} %copy.92, f32[4,4,3,128]{3,2,1,0:T(4,128)S(1)} %copy.93), kind=kLoop, calls=%fused_computation.4.clone.1 | loop fusion | flops 2097152 | bytes 1097728 | tf_op jit(solution)/shard_map/while/body/eval_jaxpr/reduce_sum | solution.py:47
  34.5 1.9 %fusion.63 = f32[4,4,3,128]{3,2,1,0:T(4,128)S(1)} fusion(f32[4,4,128,128]{3,2,1,0:T(8,128)S(1)} %multiply_multiply_fusion.5, f32[4,4,3,128]{3,2,1,0:T(4,128)S(1)} %copy.92, f32[4,4,3,128]{3,2,1,0:T(4,128)S(1)} %copy.93), kind=kLoop, calls=%fused_computation.5.clone.1 | loop fusion | flops 2353152 | bytes 1122304 | tf_op jit(solution)/shard_map/while/body/eval_jaxpr/reduce_sum | solution.py:54
  36.4 1.0 %fusion.62 = f32[4,4,128,128]{3,2,1,0:T(8,128)S(1)} fusion(f32[4,4,3,128]{3,2,1,0:T(4,128)S(1)} %copy.92, f32[4,4,3,128]{3,2,1,0:T(4,128)S(1)} %copy.93), kind=kLoop, calls=%fused_computation.4.clone.1 | loop fusion | flops 2097152 | bytes 1097728 | tf_op jit(solution)/shard_map/while/body/eval_jaxpr/reduce_sum | solution.py:47
  37.8 1.9 %fusion.63 = f32[4,4,3,128]{3,2,1,0:T(4,128)S(1)} fusion(f32[4,4,128,128]{3,2,1,0:T(8,128)S(1)} %multiply_multiply_fusion.5, f32[4,4,3,128]{3,2,1,0:T(4,128)S(1)} %copy.92, f32[4,4,3,128]{3,2,1,0:T(4,128)S(1)} %copy.93), kind=kLoop, calls=%fused_computation.5.clone.1 | loop fusion | flops 2353152 | bytes 1122304 | tf_op jit(solution)/shard_map/while/body/eval_jaxpr/reduce_sum | solution.py:54
  39.8 1.0 %fusion.62 = f32[4,4,128,128]{3,2,1,0:T(8,128)S(1)} fusion(f32[4,4,3,128]{3,2,1,0:T(4,128)S(1)} %copy.92, f32[4,4,3,128]{3,2,1,0:T(4,128)S(1)} %copy.93), kind=kLoop, calls=%fused_computation.4.clone.1 | loop fusion | flops 2097152 | bytes 1097728 | tf_op jit(solution)/shard_map/while/body/eval_jaxpr/reduce_sum | solution.py:47
  41.2 1.9 %fusion.63 = f32[4,4,3,128]{3,2,1,0:T(4,128)S(1)} fusion(f32[4,4,128,128]{3,2,1,0:T(8,128)S(1)} %multiply_multiply_fusion.5, f32[4,4,3,128]{3,2,1,0:T(4,128)S(1)} %copy.92, f32[4,4,3,128]{3,2,1,0:T(4,128)S(1)} %copy.93), kind=kLoop, calls=%fused_computation.5.clone.1 | loop fusion | flops 2353152 | bytes 1122304 | tf_op jit(solution)/shard_map/while/body/eval_jaxpr/reduce_sum | solution.py:54
  43.2 1.0 %fusion.62 = f32[4,4,128,128]{3,2,1,0:T(8,128)S(1)} fusion(f32[4,4,3,128]{3,2,1,0:T(4,128)S(1)} %copy.92, f32[4,4,3,128]{3,2,1,0:T(4,128)S(1)} %copy.93), kind=kLoop, calls=%fused_computation.4.clone.1 | loop fusion | flops 2097152 | bytes 1097728 | tf_op jit(solution)/shard_map/while/body/eval_jaxpr/reduce_sum | solution.py:47
  44.6 1.9 %fusion.63 = f32[4,4,3,128]{3,2,1,0:T(4,128)S(1)} fusion(f32[4,4,128,128]{3,2,1,0:T(8,128)S(1)} %multiply_multiply_fusion.5, f32[4,4,3,128]{3,2,1,0:T(4,128)S(1)} %copy.92, f32[4,4,3,128]{3,2,1,0:T(4,128)S(1)} %copy.93), kind=kLoop, calls=%fused_computation.5.clone.1 | loop fusion | flops 2353152 | bytes 1122304 | tf_op jit(solution)/shard_map/while/body/eval_jaxpr/reduce_sum | solution.py:54
  46.8 0.9 %copy.73 = f32[4,3,1024]{0,1,2:T(4,128)S(1)} copy(f32[4,3,1024]{2,0,1:T(4,128)S(1)} %add.36) | data formatting | bytes 98304 | tf_op jit(solution)/shard_map/add | solution.py:119
  47.7 1.9 %reshape.222 = f32[8,1,1536]{2,1,0:T(1,128)} reshape(f32[1024,3,4]{2,1,0:T(4,128)S(1)} %bitcast.86) | data formatting | bytes 98304
  49.6 5.1 %all-to-all-start.1 = ((f32[8,1,1536]{2,1,0:T(1,128)}), f32[8,1,1536]{2,1,0:T(1,128)S(1)}, u32[]{:S(2)}, u32[]{:S(2)}) async-start(f32[8,1,1536]{2,1,0:T(1,128)} %reshape.222), calls=%async_computation.1 | async-start | bytes 98304 | tf_op jit(solution)/shard_map/all_to_all | solution.py:120
  56.0 1.2 %reshape.225 = f32[1024,3,4]{2,1,0:T(4,128)S(1)} reshape(f32[8,1536]{1,0:T(8,128)S(1)} %reduce.1) | data formatting | bytes 98304
  57.9 2.6 %all-to-all-done.1 = f32[8,1,1536]{2,1,0:T(1,128)S(1)} async-done(((f32[8,1,1536]{2,1,0:T(1,128)}), f32[8,1,1536]{2,1,0:T(1,128)S(1)}, u32[]{:S(2)}, u32[]{:S(2)}) %all-to-all-start.1) | async-done | bytes 49184 | tf_op jit(solution)/shard_map/all_to_all | solution.py:120
  61.3 1.2 %reshape.223 = f32[1024,3,4]{2,1,0:T(4,128)S(1)} reshape(f32[8,1536]{1,0:T(8,128)S(1)} %reduce) | data formatting | bytes 98304
  65.1 3.4 %all-to-all-start.2 = ((f32[32,2,3,128]{3,1,2,0:T(2,128)}), f32[32,2,3,128]{3,1,2,0:T(2,128)S(1)}, u32[]{:S(2)}, u32[]{:S(2)}) async-start(f32[32,2,3,128]{3,1,2,0:T(2,128)} %copy.76), calls=%async_computation.2 | async-start | bytes 196608 | tf_op jit(solution)/shard_map/all_to_all | solution.py:127
  68.5 12.1 %all-gather = f32[8,1,128]{2,1,0:T(1,128)S(1)} all-gather(f32[1,1,128]{2,1,0:T(1,128)S(1)} %multiply_bitcast_fusion), channel_id=1, replica_groups=mesh['bead'=8,'atom'=4] {'bead'}, dimensions={0}, use_global_device_ids=true | all-gather | bytes 4608 | tf_op jit(solution)/shard_map/all_gather | solution.py:128
  (114 shorter events, 13.7 us)
Async XLA Ops:
  2.1 12.8 %copy-start.2 = (s32[32]{0:T(128)S(1)}, s32[32]{0:T(128)}, u32[]{:S(2)}) copy-start(s32[32]{0:T(128)} %param.15) | copy-start | bytes 388
  2.1 13.8 %copy-start.3 = (s32[32]{0:T(128)S(1)}, s32[32]{0:T(128)}, u32[]{:S(2)}) copy-start(s32[32]{0:T(128)} %param.16) | copy-start | bytes 388
  2.2 14.7 %copy-start = (f32[4,3,1024]{2,0,1:T(4,128)S(1)}, f32[4,3,1024]{2,0,1:T(4,128)}, u32[]{:S(2)}) copy-start(f32[4,3,1024]{2,0,1:T(4,128)} %param.11) | copy-start | bytes 147460
  2.2 14.7 %collective-permute-start = (f32[4,4,1024]{2,0,1:T(4,128)S(1)}, f32[4,4,1024]{2,0,1:T(4,128)S(1)}, u32[]{:S(2)}, u32[]{:S(2)}) collective-permute-start(f32[4,4,1024]{2,0,1:T(4,128)S(1)} %pad_maximum_fusion.3), channel_id=1, source_target_pairs={{0,1},{1,2},{2,3},{3,0},{4,5},{5,6},{6,7},{7,4},{8,9},{9,10},{10,1... | collective-permute-start | bytes 196616 | tf_op jit(solution)/shard_map/ppermute | solution.py:17
  5.2 11.7 %collective-permute-start.1 = (f32[4,4,1024]{2,0,1:T(4,128)S(1)}, f32[4,4,1024]{2,0,1:T(4,128)S(1)}, u32[]{:S(2)}, u32[]{:S(2)}) collective-permute-start(f32[4,4,1024]{2,0,1:T(4,128)S(1)} %pad_maximum_fusion.3), channel_id=1, source_target_pairs={{1,0},{2,1},{3,2},{0,3},{5,4},{6,5},{7,6},{4,7},{9,8},{10,9},{11,1... | collective-permute-start | bytes 196616 | tf_op jit(solution)/shard_map/ppermute | solution.py:20
  9.7 39.9 %all-to-all-start = ((f32[8,1,1536]{2,1,0:T(1,128)}), f32[8,1,1536]{2,1,0:T(1,128)S(1)}, u32[]{:S(2)}, u32[]{:S(2)}) async-start(f32[8,1,1536]{2,1,0:T(1,128)} %reshape.224), calls=%async_computation | async-start | bytes 98304 | tf_op jit(solution)/shard_map/all_to_all | solution.py:99
  19.4 27.4 %copy-start.1 = (f32[4,3,1024]{2,0,1:T(4,128)S(1)}, f32[4,3,1024]{2,0,1:T(4,128)}, u32[]{:S(2)}) copy-start(f32[4,3,1024]{2,0,1:T(4,128)} %param.12) | copy-start | bytes 147460
  49.6 10.9 %all-to-all-start.1 = ((f32[8,1,1536]{2,1,0:T(1,128)}), f32[8,1,1536]{2,1,0:T(1,128)S(1)}, u32[]{:S(2)}, u32[]{:S(2)}) async-start(f32[8,1,1536]{2,1,0:T(1,128)} %reshape.222), calls=%async_computation.1 | async-start | bytes 98304 | tf_op jit(solution)/shard_map/all_to_all | solution.py:120
  65.1 15.5 %all-to-all-start.2 = ((f32[32,2,3,128]{3,1,2,0:T(2,128)}), f32[32,2,3,128]{3,1,2,0:T(2,128)S(1)}, u32[]{:S(2)}, u32[]{:S(2)}) async-start(f32[32,2,3,128]{3,1,2,0:T(2,128)} %copy.76), calls=%async_computation.2 | async-start | bytes 196608 | tf_op jit(solution)/shard_map/all_to_all | solution.py:127
where the time goes:
time: 82.5 us; the launch traced here: 81.9 us
  other arithmetic  30.1 us (36%)
  starting transfers between devices  17.8 us (22%)
  local copies, waits for them, and re-layouts  15.6 us (19%)
  blocking collectives  12.1 us (15%)
  waiting for transfers between devices  2.63 us (3%)
  between operations  1.65 us (2%)
  matrix products  1.39 us (2%)
    reduce_sum x8, other arithmetic, pair_force(): return jnp.sum(separation * weights[..., None, :, :], axis=-1)  14.9 us
    all_gather x1, blocking collectives, on_device(): spring = lax.all_gather(spring_sub, 'bead', axis=0, tiled=True)  12.1 us
    unnamed x14, local copies, waits for them, and re-layouts  8.41 us
    reduce_sum x8, other arithmetic, pair_force(): dist_sq = jnp.sum(separation * separation, axis=-3)  8.35 us
    all_to_all x1, starting transfers between devices, on_device(): lax.all_to_all(positions, 'bead', split_axis=2, concat_axis=0, tiled=True)  5.29 us
    all_to_all x1, starting transfers between devices, on_device(): lax.all_to_all(kicked, 'bead', split_axis=2, concat_axis=0, tiled=True)  5.09 us
    all_to_all x1, starting transfers between devices, on_device(): lax.all_to_all(returned_rows, 'bead', split_axis=0, concat_axis=3, tiled=...  3.36 us
    ppermute x1, starting transfers between devices, extended(): lax.ppermute(lax.slice_in_dim(block, block.shape[dim] - width, None, axis...  3.02 us
  transfers between devices with their start and end apart: 5, of which 1 were waited for; matrix products, arithmetic and copies ran while one was open for 49% of the time, Pallas kernels for 0%

commit v1 on v0

--- a/solution.py
+++ b/solution.py
@@ -96,7 +96,12 @@
     hp = lax.Precision.HIGHEST
     table, frequency = cycle_table(beads)
     sub_atoms = atom_dev // bead_count
-    gathered_pos = lax.all_to_all(positions, "bead", split_axis=2, concat_axis=0, tiled=True)
+    gathered_pos = jnp.concatenate(
+        lax.all_to_all(
+            jnp.stack(jnp.split(positions, lax.axis_size("bead"), axis=2), axis=0), "bead", 0, 0
+        ),
+        axis=0,
+    )
     charge_rows = jnp.broadcast_to(charge[None, None, :], (bead_dev, 1, atom_dev))
     packed = jnp.concatenate([positions, charge_rows], axis=1)
     haloed = extended(packed, (("atom", 2),), atom_dev)

time: 82.5 us -> 92.1 us (1.12)
  local copies, waits for them, and re-layouts: 15.6 us -> 20.5 us
  waiting for transfers between devices: 2.63 us -> 5.81 us
  other arithmetic: 30.1 us -> 31.5 us
    unnamed x14 -> x12, local copies, waits for them, and re-layouts: 8.41 us -> 12.7 us
    all_to_all x1, waiting for transfers between devices: 2.61 us -> 5.8 us  [on_device(): lax.all_to_all(kicked, 'bead', split_axis=2, concat_axis=0, tiled=True)]
    another operation x0 -> x1, local copies, waits for them, and re-layouts: none -> 1.28 us  [on_device(): jnp.stack(jnp.split(positions, lax.axis_size('bead'), axis=2), axis=0)]
  transfers between devices with their start and end apart: 5 -> 5, of which waited for: 1 -> 1; matrix products, arithmetic and copies ran while one was open for 49% -> 50% of each run, Pallas kernels for 0% -> 0%
where the time goes in v1:
time: 92.1 us; the launch traced here: 91.2 us
  other arithmetic  31.5 us (34%)
  local copies, waits for them, and re-layouts  20.5 us (22%)
  starting transfers between devices  17.8 us (19%)
  blocking collectives  12.1 us (13%)
  waiting for transfers between devices  5.81 us (6%)
  between operations  1.56 us (2%)
  matrix products  1.39 us (2%)
    reduce_sum x8, other arithmetic, pair_force(): return jnp.sum(separation * weights[..., None, :, :], axis=-1)  14.9 us
    unnamed x12, local copies, waits for them, and re-layouts  12.7 us
    all_gather x1, blocking collectives, on_device(): spring = lax.all_gather(spring_sub, 'bead', axis=0, tiled=True)  12.1 us
    reduce_sum x8, other arithmetic, pair_force(): dist_sq = jnp.sum(separation * separation, axis=-3)  8.35 us
    all_to_all x1, waiting for transfers between devices, on_device(): lax.all_to_all(kicked, 'bead', split_axis=2, concat_axis=0, tiled=True)  5.8 us
    all_to_all x1, starting transfers between devices, on_device(): lax.all_to_all(jnp.stack(jnp.split(positions, lax.axis_size('bead'), axis...  5.29 us
    all_to_all x1, starting transfers between devices, on_device(): lax.all_to_all(kicked, 'bead', split_axis=2, concat_axis=0, tiled=True)  5.1 us
    all_to_all x1, starting transfers between devices, on_device(): lax.all_to_all(returned_rows, 'bead', split_axis=0, concat_axis=3, tiled=...  3.36 us
  transfers between devices with their start and end apart: 5, of which 1 were waited for; matrix products, arithmetic and copies ran while one was open for 50% of the time, Pallas kernels for 0%

profile of v1, /device:TPU:0, one launch (start us, length us, event | category | flops | bytes accessed | tf_op | source)
XLA Modules:
  0.0 91.2 jit_solution(3047961756806299245)
XLA Ops:
  2.1 3.0 %collective-permute-start = (f32[4,4,1024]{2,0,1:T(4,128)S(1)}, f32[4,4,1024]{2,0,1:T(4,128)S(1)}, u32[]{:S(2)}, u32[]{:S(2)}) collective-permute-start(f32[4,4,1024]{2,0,1:T(4,128)S(1)} %pad_maximum_fusion.3), channel_id=1, source_target_pairs={{0,1},{1,2},{2,3},{3,0},{4,5},{5,6},{6,7},{7,4},{8,9},{9,10},{10,1... | collective-permute-start | bytes 196616 | tf_op jit(solution)/shard_map/ppermute | solution.py:17
  6.2 1.3 %constant_dynamic-update-slice_fusion.7 = f32[8,4,3,128]{3,1,2,0:T(4,128)} fusion(f32[4,3,1024]{2,0,1:T(4,128)} %param.11), kind=kLoop, calls=%fused_computation.41 | loop fusion | bytes 12288
  7.5 1.3 %constant_dynamic-update-slice_fusion.6 = f32[8,4,3,128]{3,1,2,0:T(4,128)} fusion(f32[8,4,3,128]{3,1,2,0:T(4,128)} %constant_dynamic-update-slice_fusion.7, f32[4,3,1024]{2,0,1:T(4,128)} %param.11), kind=kLoop, calls=%fused_computation.40 | loop fusion | bytes 12288
  8.7 1.3 %constant_dynamic-update-slice_fusion.5 = f32[8,4,3,128]{3,1,2,0:T(4,128)} fusion(f32[8,4,3,128]{3,1,2,0:T(4,128)} %constant_dynamic-update-slice_fusion.6, f32[4,3,1024]{2,0,1:T(4,128)} %param.11), kind=kLoop, calls=%fused_computation.39 | loop fusion | bytes 12288
  10.0 1.3 %constant_dynamic-update-slice_fusion.4 = f32[8,4,3,128]{3,1,2,0:T(4,128)} fusion(f32[8,4,3,128]{3,1,2,0:T(4,128)} %constant_dynamic-update-slice_fusion.5, f32[4,3,1024]{2,0,1:T(4,128)} %param.11), kind=kLoop, calls=%fused_computation.38 | loop fusion | bytes 12288
  11.3 1.3 %constant_dynamic-update-slice_fusion.3 = f32[8,4,3,128]{3,1,2,0:T(4,128)} fusion(f32[8,4,3,128]{3,1,2,0:T(4,128)} %constant_dynamic-update-slice_fusion.4, f32[4,3,1024]{2,0,1:T(4,128)} %param.11), kind=kLoop, calls=%fused_computation.37 | loop fusion | bytes 12288
  12.6 1.3 %constant_dynamic-update-slice_fusion.2 = f32[8,4,3,128]{3,1,2,0:T(4,128)} fusion(f32[8,4,3,128]{3,1,2,0:T(4,128)} %constant_dynamic-update-slice_fusion.3, f32[4,3,1024]{2,0,1:T(4,128)} %param.11), kind=kLoop, calls=%fused_computation.36 | loop fusion | bytes 12288
  13.9 1.3 %constant_dynamic-update-slice_fusion.1 = f32[8,4,3,128]{3,1,2,0:T(4,128)} fusion(f32[8,4,3,128]{3,1,2,0:T(4,128)} %constant_dynamic-update-slice_fusion.2, f32[4,3,1024]{2,0,1:T(4,128)} %param.11), kind=kLoop, calls=%fused_computation.35 | loop fusion | bytes 12288
  15.2 1.3 %constant_dynamic-update-slice_fusion = f32[8,4,3,128]{3,1,2,0:T(4,128)} fusion(f32[8,4,3,128]{3,1,2,0:T(4,128)} %constant_dynamic-update-slice_fusion.1, f32[4,3,1024]{2,0,1:T(4,128)} %param.11), kind=kLoop, calls=%fused_computation.34 | loop fusion | bytes 12288 | tf_op jit(solution)/shard_map/stack | solution.py:101
  16.5 5.3 %all-to-all-start = ((f32[8,4,3,128]{3,1,2,0:T(4,128)}), f32[8,4,3,128]{3,1,2,0:T(4,128)S(1)}, u32[]{:S(2)}, u32[]{:S(2)}) async-start(f32[8,4,3,128]{3,1,2,0:T(4,128)} %constant_dynamic-update-slice_fusion), calls=%async_computation | async-start | bytes 98304 | tf_op jit(solution)/shard_map/all_to_all | solution.py:100
  28.2 27.1 %while.10 = (s32[]{:T(128)}, f32[8,4,4,3,128]{4,3,2,1,0:T(4,128)S(1)}, f32[8,4,2,4,4,128]{5,3,1,4,2,0:T(4,128)S(1)}, s32[]{:T(128)}) while((s32[]{:T(128)}, f32[8,4,4,3,128]{4,3,2,1,0:T(4,128)S(1)}, f32[8,4,2,4,4,128]{5,3,1,4,2,0:T(4,128)S(1)}, s32[]{:T(128)}) %tuple.41), condition=%wide.region_3.5_spmd, body=%wide.region_0.4_spmd.sunk | while | flops 5761026 | bytes 4759613 | solution.py:83
  28.3 1.0 %fusion.62 = f32[4,4,128,128]{3,2,1,0:T(8,128)S(1)} fusion(f32[4,4,3,128]{3,2,1,0:T(4,128)S(1)} %copy.89, f32[4,4,3,128]{3,2,1,0:T(4,128)S(1)} %copy.90), kind=kLoop, calls=%fused_computation.4.clone.1 | loop fusion | flops 2097152 | bytes 1097728 | tf_op jit(solution)/shard_map/while/body/eval_jaxpr/reduce_sum | solution.py:47
  29.7 1.9 %fusion.63 = f32[4,4,3,128]{3,2,1,0:T(4,128)S(1)} fusion(f32[4,4,128,128]{3,2,1,0:T(8,128)S(1)} %multiply_multiply_fusion.5, f32[4,4,3,128]{3,2,1,0:T(4,128)S(1)} %copy.89, f32[4,4,3,128]{3,2,1,0:T(4,128)S(1)} %copy.90), kind=kLoop, calls=%fused_computation.5.clone.1 | loop fusion | flops 2353152 | bytes 1122304 | tf_op jit(solution)/shard_map/while/body/eval_jaxpr/reduce_sum | solution.py:54
  31.7 1.0 %fusion.62 = f32[4,4,128,128]{3,2,1,0:T(8,128)S(1)} fusion(f32[4,4,3,128]{3,2,1,0:T(4,128)S(1)} %copy.89, f32[4,4,3,128]{3,2,1,0:T(4,128)S(1)} %copy.90), kind=kLoop, calls=%fused_computation.4.clone.1 | loop fusion | flops 2097152 | bytes 1097728 | tf_op jit(solution)/shard_map/while/body/eval_jaxpr/reduce_sum | solution.py:47
  33.1 1.9 %fusion.63 = f32[4,4,3,128]{3,2,1,0:T(4,128)S(1)} fusion(f32[4,4,128,128]{3,2,1,0:T(8,128)S(1)} %multiply_multiply_fusion.5, f32[4,4,3,128]{3,2,1,0:T(4,128)S(1)} %copy.89, f32[4,4,3,128]{3,2,1,0:T(4,128)S(1)} %copy.90), kind=kLoop, calls=%fused_computation.5.clone.1 | loop fusion | flops 2353152 | bytes 1122304 | tf_op jit(solution)/shard_map/while/body/eval_jaxpr/reduce_sum | solution.py:54
  35.1 1.0 %fusion.62 = f32[4,4,128,128]{3,2,1,0:T(8,128)S(1)} fusion(f32[4,4,3,128]{3,2,1,0:T(4,128)S(1)} %copy.89, f32[4,4,3,128]{3,2,1,0:T(4,128)S(1)} %copy.90), kind=kLoop, calls=%fused_computation.4.clone.1 | loop fusion | flops 2097152 | bytes 1097728 | tf_op jit(solution)/shard_map/while/body/eval_jaxpr/reduce_sum | solution.py:47
  36.5 1.9 %fusion.63 = f32[4,4,3,128]{3,2,1,0:T(4,128)S(1)} fusion(f32[4,4,128,128]{3,2,1,0:T(8,128)S(1)} %multiply_multiply_fusion.5, f32[4,4,3,128]{3,2,1,0:T(4,128)S(1)} %copy.89, f32[4,4,3,128]{3,2,1,0:T(4,128)S(1)} %copy.90), kind=kLoop, calls=%fused_computation.5.clone.1 | loop fusion | flops 2353152 | bytes 1122304 | tf_op jit(solution)/shard_map/while/body/eval_jaxpr/reduce_sum | solution.py:54
  38.5 1.0 %fusion.62 = f32[4,4,128,128]{3,2,1,0:T(8,128)S(1)} fusion(f32[4,4,3,128]{3,2,1,0:T(4,128)S(1)} %copy.89, f32[4,4,3,128]{3,2,1,0:T(4,128)S(1)} %copy.90), kind=kLoop, calls=%fused_computation.4.clone.1 | loop fusion | flops 2097152 | bytes 1097728 | tf_op jit(solution)/shard_map/while/body/eval_jaxpr/reduce_sum | solution.py:47
  39.9 1.9 %fusion.63 = f32[4,4,3,128]{3,2,1,0:T(4,128)S(1)} fusion(f32[4,4,128,128]{3,2,1,0:T(8,128)S(1)} %multiply_multiply_fusion.5, f32[4,4,3,128]{3,2,1,0:T(4,128)S(1)} %copy.89, f32[4,4,3,128]{3,2,1,0:T(4,128)S(1)} %copy.90), kind=kLoop, calls=%fused_computation.5.clone.1 | loop fusion | flops 2353152 | bytes 1122304 | tf_op jit(solution)/shard_map/while/body/eval_jaxpr/reduce_sum | solution.py:54
  41.9 1.0 %fusion.62 = f32[4,4,128,128]{3,2,1,0:T(8,128)S(1)} fusion(f32[4,4,3,128]{3,2,1,0:T(4,128)S(1)} %copy.89, f32[4,4,3,128]{3,2,1,0:T(4,128)S(1)} %copy.90), kind=kLoop, calls=%fused_computation.4.clone.1 | loop fusion | flops 2097152 | bytes 1097728 | tf_op jit(solution)/shard_map/while/body/eval_jaxpr/reduce_sum | solution.py:47
  43.3 1.9 %fusion.63 = f32[4,4,3,128]{3,2,1,0:T(4,128)S(1)} fusion(f32[4,4,128,128]{3,2,1,0:T(8,128)S(1)} %multiply_multiply_fusion.5, f32[4,4,3,128]{3,2,1,0:T(4,128)S(1)} %copy.89, f32[4,4,3,128]{3,2,1,0:T(4,128)S(1)} %copy.90), kind=kLoop, calls=%fused_computation.5.clone.1 | loop fusion | flops 2353152 | bytes 1122304 | tf_op jit(solution)/shard_map/while/body/eval_jaxpr/reduce_sum | solution.py:54
  45.3 1.0 %fusion.62 = f32[4,4,128,128]{3,2,1,0:T(8,128)S(1)} fusion(f32[4,4,3,128]{3,2,1,0:T(4,128)S(1)} %copy.89, f32[4,4,3,128]{3,2,1,0:T(4,128)S(1)} %copy.90), kind=kLoop, calls=%fused_computation.4.clone.1 | loop fusion | flops 2097152 | bytes 1097728 | tf_op jit(solution)/shard_map/while/body/eval_jaxpr/reduce_sum | solution.py:47
  46.7 1.9 %fusion.63 = f32[4,4,3,128]{3,2,1,0:T(4,128)S(1)} fusion(f32[4,4,128,128]{3,2,1,0:T(8,128)S(1)} %multiply_multiply_fusion.5, f32[4,4,3,128]{3,2,1,0:T(4,128)S(1)} %copy.89, f32[4,4,3,128]{3,2,1,0:T(4,128)S(1)} %copy.90), kind=kLoop, calls=%fused_computation.5.clone.1 | loop fusion | flops 2353152 | bytes 1122304 | tf_op jit(solution)/shard_map/while/body/eval_jaxpr/reduce_sum | solution.py:54
  48.7 1.0 %fusion.62 = f32[4,4,128,128]{3,2,1,0:T(8,128)S(1)} fusion(f32[4,4,3,128]{3,2,1,0:T(4,128)S(1)} %copy.89, f32[4,4,3,128]{3,2,1,0:T(4,128)S(1)} %copy.90), kind=kLoop, calls=%fused_computation.4.clone.1 | loop fusion | flops 2097152 | bytes 1097728 | tf_op jit(solution)/shard_map/while/body/eval_jaxpr/reduce_sum | solution.py:47
  50.1 1.9 %fusion.63 = f32[4,4,3,128]{3,2,1,0:T(4,128)S(1)} fusion(f32[4,4,128,128]{3,2,1,0:T(8,128)S(1)} %multiply_multiply_fusion.5, f32[4,4,3,128]{3,2,1,0:T(4,128)S(1)} %copy.89, f32[4,4,3,128]{3,2,1,0:T(4,128)S(1)} %copy.90), kind=kLoop, calls=%fused_computation.5.clone.1 | loop fusion | flops 2353152 | bytes 1122304 | tf_op jit(solution)/shard_map/while/body/eval_jaxpr/reduce_sum | solution.py:54
  53.5 1.9 %fusion.63 = f32[4,4,3,128]{3,2,1,0:T(4,128)S(1)} fusion(f32[4,4,128,128]{3,2,1,0:T(8,128)S(1)} %multiply_multiply_fusion.5, f32[4,4,3,128]{3,2,1,0:T(4,128)S(1)} %copy.89, f32[4,4,3,128]{3,2,1,0:T(4,128)S(1)} %copy.90), kind=kLoop, calls=%fused_computation.5.clone.1 | loop fusion | flops 2353152 | bytes 1122304 | tf_op jit(solution)/shard_map/while/body/eval_jaxpr/reduce_sum | solution.py:54
  56.5 1.9 %reshape.226 = f32[8,1,1536]{2,1,0:T(1,128)} reshape(f32[1024,3,4]{2,1,0:T(4,128)S(1)} %bitcast.97) | data formatting | bytes 98304
  58.4 5.1 %all-to-all-start.1 = ((f32[8,1,1536]{2,1,0:T(1,128)}), f32[8,1,1536]{2,1,0:T(1,128)S(1)}, u32[]{:S(2)}, u32[]{:S(2)}) async-start(f32[8,1,1536]{2,1,0:T(1,128)} %reshape.226), calls=%async_computation.1 | async-start | bytes 98304 | tf_op jit(solution)/shard_map/all_to_all | solution.py:125
  63.5 5.8 %all-to-all-done.1 = f32[8,1,1536]{2,1,0:T(1,128)S(1)} async-done(((f32[8,1,1536]{2,1,0:T(1,128)}), f32[8,1,1536]{2,1,0:T(1,128)S(1)}, u32[]{:S(2)}, u32[]{:S(2)}) %all-to-all-start.1) | async-done | bytes 49184 | tf_op jit(solution)/shard_map/all_to_all | solution.py:125
  70.6 1.2 %reshape.227 = f32[1024,3,4]{2,1,0:T(4,128)S(1)} reshape(f32[8,1536]{1,0:T(8,128)S(1)} %reduce) | data formatting | bytes 98304
  74.4 3.4 %all-to-all-start.2 = ((f32[32,2,3,128]{3,1,2,0:T(2,128)}), f32[32,2,3,128]{3,1,2,0:T(2,128)S(1)}, u32[]{:S(2)}, u32[]{:S(2)}) async-start(f32[32,2,3,128]{3,1,2,0:T(2,128)} %copy.73), calls=%async_computation.2 | async-start | bytes 196608 | tf_op jit(solution)/shard_map/all_to_all | solution.py:132
  77.8 12.1 %all-gather = f32[8,1,128]{2,1,0:T(1,128)S(1)} all-gather(f32[1,1,128]{2,1,0:T(1,128)S(1)} %multiply_bitcast_fusion), channel_id=1, replica_groups=mesh['bead'=8,'atom'=4] {'bead'}, dimensions={0}, use_global_device_ids=true | all-gather | bytes 4608 | tf_op jit(solution)/shard_map/all_gather | solution.py:133
  (111 shorter events, 18.8 us)
Async XLA Ops:
  2.1 22.8 %collective-permute-start = (f32[4,4,1024]{2,0,1:T(4,128)S(1)}, f32[4,4,1024]{2,0,1:T(4,128)S(1)}, u32[]{:S(2)}, u32[]{:S(2)}) collective-permute-start(f32[4,4,1024]{2,0,1:T(4,128)S(1)} %pad_maximum_fusion.3), channel_id=1, source_target_pairs={{0,1},{1,2},{2,3},{3,0},{4,5},{5,6},{6,7},{7,4},{8,9},{9,10},{10,1... | collective-permute-start | bytes 196616 | tf_op jit(solution)/shard_map/ppermute | solution.py:17
  5.2 19.7 %collective-permute-start.1 = (f32[4,4,1024]{2,0,1:T(4,128)S(1)}, f32[4,4,1024]{2,0,1:T(4,128)S(1)}, u32[]{:S(2)}, u32[]{:S(2)}) collective-permute-start(f32[4,4,1024]{2,0,1:T(4,128)S(1)} %pad_maximum_fusion.3), channel_id=1, source_target_pairs={{1,0},{2,1},{3,2},{0,3},{5,4},{6,5},{7,6},{4,7},{9,8},{10,9},{11,1... | collective-permute-start | bytes 196616 | tf_op jit(solution)/shard_map/ppermute | solution.py:20
  16.5 42.0 %all-to-all-start = ((f32[8,4,3,128]{3,1,2,0:T(4,128)}), f32[8,4,3,128]{3,1,2,0:T(4,128)S(1)}, u32[]{:S(2)}, u32[]{:S(2)}) async-start(f32[8,4,3,128]{3,1,2,0:T(4,128)} %constant_dynamic-update-slice_fusion), calls=%async_computation | async-start | bytes 98304 | tf_op jit(solution)/shard_map/all_to_all | solution.py:100
  28.2 27.4 %copy-start = (f32[4,3,1024]{2,0,1:T(4,128)S(1)}, f32[4,3,1024]{2,0,1:T(4,128)}, u32[]{:S(2)}) copy-start(f32[4,3,1024]{2,0,1:T(4,128)} %param.12) | copy-start | bytes 147460
  58.4 10.9 %all-to-all-start.1 = ((f32[8,1,1536]{2,1,0:T(1,128)}), f32[8,1,1536]{2,1,0:T(1,128)S(1)}, u32[]{:S(2)}, u32[]{:S(2)}) async-start(f32[8,1,1536]{2,1,0:T(1,128)} %reshape.226), calls=%async_computation.1 | async-start | bytes 98304 | tf_op jit(solution)/shard_map/all_to_all | solution.py:125
  74.4 15.5 %all-to-all-start.2 = ((f32[32,2,3,128]{3,1,2,0:T(2,128)}), f32[32,2,3,128]{3,1,2,0:T(2,128)S(1)}, u32[]{:S(2)}, u32[]{:S(2)}) async-start(f32[32,2,3,128]{3,1,2,0:T(2,128)} %copy.73), calls=%async_computation.2 | async-start | bytes 196608 | tf_op jit(solution)/shard_map/all_to_all | solution.py:132
